TPU v7x, 32 devices: a whole 2x2x4 slice. The times are simulated.
32 devices in a mesh: pair: 2 (over y), rep: 4 (over x, core), blk: 4 (over z).
Axes of the slice: x: 2, y: 2, z: 4, core: 2. Of those that a mesh axis runs over, the one named last changes fastest.
Arguments:
- src_spectra: bfloat16 [64, 8192], P(None, ('pair', 'rep', 'blk')), parts along dimension 1, may hold values from -4 to 4
- tgt_spectra: bfloat16 [64, 8192], P(None, ('pair', 'blk')), parts along dimension 1, may hold values from -4 to 4
- log_src_weight: float32 [8192], P(('pair', 'rep', 'blk')), parts along dimension 0, may hold values from -2 to 2
- log_tgt_weight: float32 [8192], P(('pair', 'blk')), parts along dimension 0, may hold values from -2 to 2
- src_potential: float32 [8192], P(('pair', 'rep', 'blk')), parts along dimension 0, may hold values from -4 to 250
- tgt_potential: float32 [8192], P(('pair', 'blk')), parts along dimension 0, may hold values from -4 to 250
Outputs:
- src_updated: float32 [8192], P(('pair', 'rep', 'blk')), parts along dimension 0
- tgt_updated: float32 [8192], P(('pair', 'blk')), parts along dimension 0
There are 2 independent parts, one for each index of `pair`. A program takes and returns all parts, laid end to end along the dimension named above; each array names one. Nothing has to cross between parts.
All inputs are finite; a program needn't handle non-finite values.
Results may differ from a plain program's by a relative error of at most 0.0003.
Values may be sent and summed in bfloat16 or wider, within the bound.
No kernel may reach another device: no remote copies, remote signals or barrier semaphores. Data moves between devices by JAX's collectives and lax.ppermute only.
A program may use at most 128 MiB of HBM per device.

v0:
```python
import jax
import jax.numpy as jnp
from jax import lax
from jax.sharding import PartitionSpec as P


def passed_along(value, axis, steps):
    count = lax.axis_size(axis)
    pairs = [(source, (source + steps) % count) for source in range(count)]
    return lax.ppermute(value, axis, pairs)


def merged(value, axis, join):
    pieces = jax.tree.map(lambda part: lax.all_gather(part, axis), value)
    head = jax.tree.map(lambda part: part[0], pieces)
    tail = jax.tree.map(lambda part: part[1:], pieces)
    so_far, _ = lax.scan(lambda so_far, share: (join(so_far, share), None), head, tail)
    return so_far


def peaks_join(earlier, later):
    joined = jnp.maximum(earlier[0], later[0])
    return (
        joined,
        earlier[1] * jnp.exp(earlier[0] - joined) + later[1] * jnp.exp(later[0] - joined),
    )


def tile_scores(src_spectra, src_square, src_bias, tgt_bias, spectra_piece, offset):
    width = spectra_piece.shape[1]
    piece_float = spectra_piece.astype(jnp.float32)
    tgt_square = 0.5 * jnp.sum(piece_float * piece_float, axis=0)
    products = lax.dot_general(
        src_spectra, spectra_piece, (((0,), (0,)), ((), ())), preferred_element_type=jnp.float32
    )
    cost_tile = src_square[:, None] + tgt_square[None, :] - products
    bias_piece = lax.dynamic_slice_in_dim(tgt_bias, offset, width, 0)
    return (bias_piece[None, :] - cost_tile, src_bias[:, None] - cost_tile)


def row_update(row_peak, row_totals, row_scores):
    joined = jnp.maximum(row_peak, jnp.max(row_scores, axis=1))
    fresh = jnp.sum(jnp.exp(row_scores - joined[:, None]), axis=1)
    return (joined, row_totals * jnp.exp(row_peak - joined) + fresh)


def column_part(col_scores):
    block_peak = jnp.max(col_scores, axis=0)
    return (block_peak, jnp.sum(jnp.exp(col_scores - block_peak[None, :]), axis=0))


def on_device(
    src_spectra, tgt_spectra, log_src_weight, log_tgt_weight, src_potential, tgt_potential
):
    src_float = src_spectra.astype(jnp.float32)
    src_square = 0.5 * jnp.sum(src_float * src_float, axis=0)
    src_bias = log_src_weight + src_potential
    tgt_bias = lax.all_gather(log_tgt_weight + tgt_potential, "blk", axis=0, tiled=True)
    own_width = tgt_spectra.shape[1]
    everything = tgt_bias.shape[0]
    rows_here = src_spectra.shape[1]
    start_peak = jnp.full((rows_here,), -jnp.inf, jnp.float32)
    start_totals = jnp.zeros((rows_here,), jnp.float32)
    shards = everything // own_width
    home = lax.axis_index("blk")

    def turn(turn_index, carry):
        row_peak, row_totals, spectra_piece, carried_peak, carried_totals = carry
        offset = (home - turn_index) % shards * own_width
        row_scores, col_scores = tile_scores(
            src_spectra, src_square, src_bias, tgt_bias, spectra_piece, offset
        )
        row_peak, row_totals = row_update(row_peak, row_totals, row_scores)
        carried_peak, carried_totals = peaks_join(
            (carried_peak, carried_totals), column_part(col_scores)
        )
        spectra_piece = passed_along(spectra_piece, "blk", 1)
        carried_peak, carried_totals = passed_along((carried_peak, carried_totals), "blk", 1)
        return (row_peak, row_totals, spectra_piece, carried_peak, carried_totals)

    carry = (
        start_peak,
        start_totals,
        tgt_spectra,
        jnp.full((own_width,), -jnp.inf, jnp.float32),
        jnp.zeros((own_width,), jnp.float32),
    )
    row_peak, row_totals, returned, carried_peak, carried_totals = lax.fori_loop(
        0, shards, turn, carry
    )
    mine_peak, mine_totals = merged((carried_peak, carried_totals), "rep", peaks_join)
    tgt_new = -(mine_peak + jnp.log(mine_totals))
    src_new = -(row_peak + jnp.log(row_totals))
    return (0.5 * (src_potential + src_new), 0.5 * (tgt_potential + tgt_new))


def solution(mesh):
    placed = (
        P(None, ("pair", "rep", "blk")),
        P(None, ("pair", "blk")),
        P(("pair", "rep", "blk")),
        P(("pair", "blk")),
        P(("pair", "rep", "blk")),
        P(("pair", "blk")),
    )
    return jax.shard_map(
        on_device,
        mesh=mesh,
        in_specs=placed,
        out_specs=(P(("pair", "rep", "blk")), P(("pair", "blk"))),
        check_vma=False,
    )
```

profile of v0, /device:TPU:0, one launch (start us, length us, event | category | flops | bytes accessed | tf_op | source)
XLA Modules:
  0.0 62.2 jit_solution(9020351512151376552)
XLA Ops:
  0.7 0.7 %copy-done.3 = f32[1024]{0:T(1024)S(1)} copy-done((f32[1024]{0:T(1024)S(1)}, f32[1024]{0:T(1024)}, u32[]{:S(2)}) %copy-start.3) | copy-done | bytes 4120
  1.4 14.9 %all_gather.15 = f32[4096]{0:T(1024)S(1)} all-gather(f32[1024]{0:T(1024)S(1)} %add.130), channel_id=1, replica_groups=mesh['pair'=2,'rep'=4,'blk'=4] {'blk'}, dimensions={0}, use_global_device_ids=true | all-gather | bytes 20480 | tf_op jit(solution)/shard_map/all_gather | solution.py:58
  16.4 0.7 %copy-done.6 = f32[256]{0:T(256)S(1)} copy-done((f32[256]{0:T(256)S(1)}, f32[256]{0:T(256)}, u32[]{:S(2)}) %copy-start.6) | copy-done | bytes 1048
  17.0 32.7 %while.37 = (s32[]{:T(128)}, f32[256]{0:T(256)S(1)}, f32[256]{0:T(256)S(1)}, bf16[64,1024]{1,0:T(8,128)(2,1)S(1)}, f32[1024]{0:T(1024)S(1)}, /*index=5*/f32[1024...) while((s32[]{:T(128)}, f32[256]{0:T(256)S(1)}, ...), condition=%wide.region_7.8_spmd.clone, body=%wide.region_1.7_spmd.clone.sunk | while | flops 36902160 | bytes 3297739 | solution.py:88
  17.1 1.6 %collective-permute-start = (bf16[64,1024]{1,0:T(8,128)(2,1)S(1)}, bf16[64,1024]{1,0:T(8,128)(2,1)S(1)}, u32[]{:S(2)}, u32[]{:S(2)}) collective-permute-start(bf16[64,1024]{1,0:T(8,128)(2,1)S(1)} %copy.17), channel_id=1, source_target_pairs={{0,1},{1,2},{2,3},{3,0},{4,5},{5,6},{6,7},{7,4},{8,9},{9,10},{10,1... | collective-permute-start | bytes 393224 | tf_op jit(solution)/shard_map/while/body/eval_jaxpr/ppermute | solution.py:10
  18.8 0.5 subtract_reduce_fusion.3
  19.3 0.4 exponential_reduce_fusion.3
  19.8 2.9 %collective-permute-start.2 = (f32[1024]{0:T(1024)S(1)}, f32[1024]{0:T(1024)S(1)}, u32[]{:S(2)}, u32[]{:S(2)}) collective-permute-start(f32[1024]{0:T(1024)S(1)} %get-tuple-element.502), channel_id=1, source_target_pairs={{0,1},{1,2},{2,3},{3,0},{4,5},{5,6},{6,7},{7,4},{8,9},{9,10},{10,1... | collective-permute-start | bytes 12296 | tf_op jit(solution)/shard_map/while/body/eval_jaxpr/ppermute | solution.py:10
  22.8 2.4 %collective-permute-done.1 = f32[1024]{0:T(1024)S(1)} collective-permute-done((f32[1024]{0:T(1024)S(1)}, f32[1024]{0:T(1024)S(1)}, u32[]{:S(2)}, u32[]{:S(2)}) %collective-permute-start.1) | collective-permute-done | bytes 4128 | tf_op jit(solution)/shard_map/while/body/eval_jaxpr/ppermute | solution.py:10
  25.3 1.1 %collective-permute-start = (bf16[64,1024]{1,0:T(8,128)(2,1)S(1)}, bf16[64,1024]{1,0:T(8,128)(2,1)S(1)}, u32[]{:S(2)}, u32[]{:S(2)}) collective-permute-start(bf16[64,1024]{1,0:T(8,128)(2,1)S(1)} %copy.17), channel_id=1, source_target_pairs={{0,1},{1,2},{2,3},{3,0},{4,5},{5,6},{6,7},{7,4},{8,9},{9,10},{10,1... | collective-permute-start | bytes 393224 | tf_op jit(solution)/shard_map/while/body/eval_jaxpr/ppermute | solution.py:10
  26.5 0.5 subtract_reduce_fusion.3
  27.0 0.4 exponential_reduce_fusion.3
  27.5 0.5 collective-permute-start.1
  28.0 1.6 %collective-permute-start.2 = (f32[1024]{0:T(1024)S(1)}, f32[1024]{0:T(1024)S(1)}, u32[]{:S(2)}, u32[]{:S(2)}) collective-permute-start(f32[1024]{0:T(1024)S(1)} %get-tuple-element.502), channel_id=1, source_target_pairs={{0,1},{1,2},{2,3},{3,0},{4,5},{5,6},{6,7},{7,4},{8,9},{9,10},{10,1... | collective-permute-start | bytes 12296 | tf_op jit(solution)/shard_map/while/body/eval_jaxpr/ppermute | solution.py:10
  29.6 3.4 %collective-permute-done.1 = f32[1024]{0:T(1024)S(1)} collective-permute-done((f32[1024]{0:T(1024)S(1)}, f32[1024]{0:T(1024)S(1)}, u32[]{:S(2)}, u32[]{:S(2)}) %collective-permute-start.1) | collective-permute-done | bytes 4128 | tf_op jit(solution)/shard_map/while/body/eval_jaxpr/ppermute | solution.py:10
  33.0 0.4 collective-permute-done.2
  33.6 0.5 subtract_reduce_fusion.3
  34.1 0.4 exponential_reduce_fusion.3
  34.6 1.6 %collective-permute-start.1 = (f32[1024]{0:T(1024)S(1)}, f32[1024]{0:T(1024)S(1)}, u32[]{:S(2)}, u32[]{:S(2)}) collective-permute-start(f32[1024]{0:T(1024)S(1)} %get-tuple-element.501), channel_id=1, source_target_pairs={{0,1},{1,2},{2,3},{3,0},{4,5},{5,6},{6,7},{7,4},{8,9},{9,10},{10,1... | collective-permute-start | bytes 12296 | tf_op jit(solution)/shard_map/while/body/eval_jaxpr/ppermute | solution.py:10
  36.2 1.1 %collective-permute-start.2 = (f32[1024]{0:T(1024)S(1)}, f32[1024]{0:T(1024)S(1)}, u32[]{:S(2)}, u32[]{:S(2)}) collective-permute-start(f32[1024]{0:T(1024)S(1)} %get-tuple-element.502), channel_id=1, source_target_pairs={{0,1},{1,2},{2,3},{3,0},{4,5},{5,6},{6,7},{7,4},{8,9},{9,10},{10,1... | collective-permute-start | bytes 12296 | tf_op jit(solution)/shard_map/while/body/eval_jaxpr/ppermute | solution.py:10
  37.3 3.8 %collective-permute-done.1 = f32[1024]{0:T(1024)S(1)} collective-permute-done((f32[1024]{0:T(1024)S(1)}, f32[1024]{0:T(1024)S(1)}, u32[]{:S(2)}, u32[]{:S(2)}) %collective-permute-start.1) | collective-permute-done | bytes 4128 | tf_op jit(solution)/shard_map/while/body/eval_jaxpr/ppermute | solution.py:10
  41.1 0.5 collective-permute-done.2
  41.8 0.5 subtract_reduce_fusion.3
  42.3 0.4 exponential_reduce_fusion.3
  42.8 1.6 %collective-permute-start.1 = (f32[1024]{0:T(1024)S(1)}, f32[1024]{0:T(1024)S(1)}, u32[]{:S(2)}, u32[]{:S(2)}) collective-permute-start(f32[1024]{0:T(1024)S(1)} %get-tuple-element.501), channel_id=1, source_target_pairs={{0,1},{1,2},{2,3},{3,0},{4,5},{5,6},{6,7},{7,4},{8,9},{9,10},{10,1... | collective-permute-start | bytes 12296 | tf_op jit(solution)/shard_map/while/body/eval_jaxpr/ppermute | solution.py:10
  44.4 4.1 %collective-permute-done.1 = f32[1024]{0:T(1024)S(1)} collective-permute-done((f32[1024]{0:T(1024)S(1)}, f32[1024]{0:T(1024)S(1)}, u32[]{:S(2)}, u32[]{:S(2)}) %collective-permute-start.1) | collective-permute-done | bytes 4128 | tf_op jit(solution)/shard_map/while/body/eval_jaxpr/ppermute | solution.py:10
  48.5 1.2 %collective-permute-done.2 = f32[1024]{0:T(1024)S(1)} collective-permute-done((f32[1024]{0:T(1024)S(1)}, f32[1024]{0:T(1024)S(1)}, u32[]{:S(2)}, u32[]{:S(2)}) %collective-permute-start.2) | collective-permute-done | bytes 4128 | tf_op jit(solution)/shard_map/while/body/eval_jaxpr/ppermute | solution.py:10
  49.7 5.2 %all-gather = f32[4096]{0:T(1024)S(1)} all-gather(f32[1024]{0:T(1024)S(1)} %get-tuple-element.300), channel_id=2, replica_groups=mesh['pair'=2,'rep'=4,'blk'=4] {'rep'}, dimensions={0}, use_global_device_ids=true | all-gather | bytes 20480 | tf_op jit(solution)/shard_map/all_gather | solution.py:14
  54.9 5.2 %all-gather.1 = f32[4096]{0:T(1024)S(1)} all-gather(f32[1024]{0:T(1024)S(1)} %get-tuple-element.301), channel_id=3, replica_groups=mesh['pair'=2,'rep'=4,'blk'=4] {'rep'}, dimensions={0}, use_global_device_ids=true | all-gather | bytes 20480 | tf_op jit(solution)/shard_map/all_gather | solution.py:14
  60.2 0.7 %slice-done = f32[1024]{0:T(1024)S(1)} async-done(((f32[4096]{0:T(1024)}), f32[1024]{0:T(1024)S(1)}, s32[]{:S(2)}) %slice-start) | async-done | bytes 4120 | tf_op jit(solution)/shard_map/slice | solution.py:15
  61.0 0.6 add_multiply_fusion
  61.6 0.6 add_multiply_fusion.1
  (74 shorter events, 1.1 us)
Async XLA Ops:
  0.6 16.4 %copy-start = (bf16[64,1024]{1,0:T(8,128)(2,1)S(1)}, bf16[64,1024]{1,0:T(8,128)(2,1)}, u32[]{:S(2)}) copy-start(bf16[64,1024]{1,0:T(8,128)(2,1)} %param.11) | copy-start | bytes 393220
  0.6 0.7 %copy-start.3 = (f32[1024]{0:T(1024)S(1)}, f32[1024]{0:T(1024)}, u32[]{:S(2)}) copy-start(f32[1024]{0:T(1024)} %param.15) | copy-start | bytes 12292
  0.7 0.7 %copy-start.4 = (f32[1024]{0:T(1024)S(1)}, f32[1024]{0:T(1024)}, u32[]{:S(2)}) copy-start(f32[1024]{0:T(1024)} %param.13) | copy-start | bytes 12292
  0.7 15.6 %copy-start.2 = (bf16[64,256]{1,0:T(8,128)(2,1)S(1)}, bf16[64,256]{1,0:T(8,128)(2,1)}, u32[]{:S(2)}) copy-start(bf16[64,256]{1,0:T(8,128)(2,1)} %param.10) | copy-start | bytes 98308
  16.3 0.7 %copy-start.6 = (f32[256]{0:T(256)S(1)}, f32[256]{0:T(256)}, u32[]{:S(2)}) copy-start(f32[256]{0:T(256)} %param.12) | copy-start | bytes 3076
  16.3 0.7 %copy-start.5 = (f32[256]{0:T(256)S(1)}, f32[256]{0:T(256)}, u32[]{:S(2)}) copy-start(f32[256]{0:T(256)} %param.14) | copy-start | bytes 3076
  17.1 8.2 %collective-permute-start = (bf16[64,1024]{1,0:T(8,128)(2,1)S(1)}, bf16[64,1024]{1,0:T(8,128)(2,1)S(1)}, u32[]{:S(2)}, u32[]{:S(2)}) collective-permute-start(bf16[64,1024]{1,0:T(8,128)(2,1)S(1)} %copy.17), channel_id=1, source_target_pairs={{0,1},{1,2},{2,3},{3,0},{4,5},{5,6},{6,7},{7,4},{8,9},{9,10},{10,1... | collective-permute-start | bytes 393224 | tf_op jit(solution)/shard_map/while/body/eval_jaxpr/ppermute | solution.py:10
  19.8 5.5 %collective-permute-start.1 = (f32[1024]{0:T(1024)S(1)}, f32[1024]{0:T(1024)S(1)}, u32[]{:S(2)}, u32[]{:S(2)}) collective-permute-start(f32[1024]{0:T(1024)S(1)} %get-tuple-element.501), channel_id=1, source_target_pairs={{0,1},{1,2},{2,3},{3,0},{4,5},{5,6},{6,7},{7,4},{8,9},{9,10},{10,1... | collective-permute-start | bytes 12296 | tf_op jit(solution)/shard_map/while/body/eval_jaxpr/ppermute | solution.py:10
  19.8 5.5 %collective-permute-start.2 = (f32[1024]{0:T(1024)S(1)}, f32[1024]{0:T(1024)S(1)}, u32[]{:S(2)}, u32[]{:S(2)}) collective-permute-start(f32[1024]{0:T(1024)S(1)} %get-tuple-element.502), channel_id=1, source_target_pairs={{0,1},{1,2},{2,3},{3,0},{4,5},{5,6},{6,7},{7,4},{8,9},{9,10},{10,1... | collective-permute-start | bytes 12296 | tf_op jit(solution)/shard_map/while/body/eval_jaxpr/ppermute | solution.py:10
  25.3 8.1 %collective-permute-start = (bf16[64,1024]{1,0:T(8,128)(2,1)S(1)}, bf16[64,1024]{1,0:T(8,128)(2,1)S(1)}, u32[]{:S(2)}, u32[]{:S(2)}) collective-permute-start(bf16[64,1024]{1,0:T(8,128)(2,1)S(1)} %copy.17), channel_id=1, source_target_pairs={{0,1},{1,2},{2,3},{3,0},{4,5},{5,6},{6,7},{7,4},{8,9},{9,10},{10,1... | collective-permute-start | bytes 393224 | tf_op jit(solution)/shard_map/while/body/eval_jaxpr/ppermute | solution.py:10
  27.5 5.5 %collective-permute-start.1 = (f32[1024]{0:T(1024)S(1)}, f32[1024]{0:T(1024)S(1)}, u32[]{:S(2)}, u32[]{:S(2)}) collective-permute-start(f32[1024]{0:T(1024)S(1)} %get-tuple-element.501), channel_id=1, source_target_pairs={{0,1},{1,2},{2,3},{3,0},{4,5},{5,6},{6,7},{7,4},{8,9},{9,10},{10,1... | collective-permute-start | bytes 12296 | tf_op jit(solution)/shard_map/while/body/eval_jaxpr/ppermute | solution.py:10
  28.0 5.4 %collective-permute-start.2 = (f32[1024]{0:T(1024)S(1)}, f32[1024]{0:T(1024)S(1)}, u32[]{:S(2)}, u32[]{:S(2)}) collective-permute-start(f32[1024]{0:T(1024)S(1)} %get-tuple-element.502), channel_id=1, source_target_pairs={{0,1},{1,2},{2,3},{3,0},{4,5},{5,6},{6,7},{7,4},{8,9},{9,10},{10,1... | collective-permute-start | bytes 12296 | tf_op jit(solution)/shard_map/while/body/eval_jaxpr/ppermute | solution.py:10
  33.4 8.2 %collective-permute-start = (bf16[64,1024]{1,0:T(8,128)(2,1)S(1)}, bf16[64,1024]{1,0:T(8,128)(2,1)S(1)}, u32[]{:S(2)}, u32[]{:S(2)}) collective-permute-start(bf16[64,1024]{1,0:T(8,128)(2,1)S(1)} %copy.17), channel_id=1, source_target_pairs={{0,1},{1,2},{2,3},{3,0},{4,5},{5,6},{6,7},{7,4},{8,9},{9,10},{10,1... | collective-permute-start | bytes 393224 | tf_op jit(solution)/shard_map/while/body/eval_jaxpr/ppermute | solution.py:10
  34.6 6.5 %collective-permute-start.1 = (f32[1024]{0:T(1024)S(1)}, f32[1024]{0:T(1024)S(1)}, u32[]{:S(2)}, u32[]{:S(2)}) collective-permute-start(f32[1024]{0:T(1024)S(1)} %get-tuple-element.501), channel_id=1, source_target_pairs={{0,1},{1,2},{2,3},{3,0},{4,5},{5,6},{6,7},{7,4},{8,9},{9,10},{10,1... | collective-permute-start | bytes 12296 | tf_op jit(solution)/shard_map/while/body/eval_jaxpr/ppermute | solution.py:10
  36.2 5.4 %collective-permute-start.2 = (f32[1024]{0:T(1024)S(1)}, f32[1024]{0:T(1024)S(1)}, u32[]{:S(2)}, u32[]{:S(2)}) collective-permute-start(f32[1024]{0:T(1024)S(1)} %get-tuple-element.502), channel_id=1, source_target_pairs={{0,1},{1,2},{2,3},{3,0},{4,5},{5,6},{6,7},{7,4},{8,9},{9,10},{10,1... | collective-permute-start | bytes 12296 | tf_op jit(solution)/shard_map/while/body/eval_jaxpr/ppermute | solution.py:10
  41.6 8.1 %collective-permute-start = (bf16[64,1024]{1,0:T(8,128)(2,1)S(1)}, bf16[64,1024]{1,0:T(8,128)(2,1)S(1)}, u32[]{:S(2)}, u32[]{:S(2)}) collective-permute-start(bf16[64,1024]{1,0:T(8,128)(2,1)S(1)} %copy.17), channel_id=1, source_target_pairs={{0,1},{1,2},{2,3},{3,0},{4,5},{5,6},{6,7},{7,4},{8,9},{9,10},{10,1... | collective-permute-start | bytes 393224 | tf_op jit(solution)/shard_map/while/body/eval_jaxpr/ppermute | solution.py:10
  42.8 5.7 %collective-permute-start.1 = (f32[1024]{0:T(1024)S(1)}, f32[1024]{0:T(1024)S(1)}, u32[]{:S(2)}, u32[]{:S(2)}) collective-permute-start(f32[1024]{0:T(1024)S(1)} %get-tuple-element.501), channel_id=1, source_target_pairs={{0,1},{1,2},{2,3},{3,0},{4,5},{5,6},{6,7},{7,4},{8,9},{9,10},{10,1... | collective-permute-start | bytes 12296 | tf_op jit(solution)/shard_map/while/body/eval_jaxpr/ppermute | solution.py:10
  44.3 5.4 %collective-permute-start.2 = (f32[1024]{0:T(1024)S(1)}, f32[1024]{0:T(1024)S(1)}, u32[]{:S(2)}, u32[]{:S(2)}) collective-permute-start(f32[1024]{0:T(1024)S(1)} %get-tuple-element.502), channel_id=1, source_target_pairs={{0,1},{1,2},{2,3},{3,0},{4,5},{5,6},{6,7},{7,4},{8,9},{9,10},{10,1... | collective-permute-start | bytes 12296 | tf_op jit(solution)/shard_map/while/body/eval_jaxpr/ppermute | solution.py:10
  54.9 5.2 %copy-start.1 = (f32[4096]{0:T(1024)}, f32[4096]{0:T(1024)S(1)}, u32[]{:S(2)}) copy-start(f32[4096]{0:T(1024)S(1)} %all-gather) | copy-start | bytes 49156
  60.2 0.7 %slice-start = ((f32[4096]{0:T(1024)}), f32[1024]{0:T(1024)S(1)}, s32[]{:S(2)}) async-start(f32[4096]{0:T(1024)} %copy-done.1), calls=%async_computation | async-start | bytes 8192 | tf_op jit(solution)/shard_map/slice | solution.py:15
where the time goes:
time: 62.4 us; the launch traced here: 62.2 us
  blocking collectives  25.3 us (41%)
  waiting for transfers between devices  16 us (26%)
  starting transfers between devices  12.2 us (20%)
  other arithmetic  3.3 us (5%)
  local copies, waits for them, and re-layouts  2.21 us (4%)
  matrix products  1.93 us (3%)
  between operations  0.73 us (1%)
    ppermute x12, waiting for transfers between devices, passed_along(): return lax.ppermute(value, axis, pairs)  16 us
    all_gather x1, blocking collectives, on_device(): lax.all_gather(log_tgt_weight + tgt_potential, 'blk', axis=0, tiled=True)  14.9 us
    ppermute x12, starting transfers between devices, passed_along(): return lax.ppermute(value, axis, pairs)  12.2 us
    all_gather x2, blocking collectives, merged(): pieces = jax.tree.map(lambda part: lax.all_gather(part, axis), value)  10.4 us
    dot_general x4, matrix products, tile_scores(): lax.dot_general(src_spectra, spectra_piece, (((0,), (0,)), ((), ())), pre...  1.93 us
    reduce_sum x4, other arithmetic, column_part(): jnp.sum(jnp.exp(col_scores - block_peak[None, :]), axis=0)  1.74 us
    unnamed x14, local copies, waits for them, and re-layouts  1.4 us
  transfers between devices with their start and end apart: 12, of which 8 were waited for; matrix products, arithmetic and copies ran while one was open for 6% of the time, Pallas kernels for 0%

commit v1 on v0

--- a/solution.py
+++ b/solution.py
@@ -2,6 +2,18 @@
 import jax.numpy as jnp
 from jax import lax
 from jax.sharding import PartitionSpec as P
+
+
+def collect(value, axis, dim):
+    ways, here = (lax.axis_size(axis), lax.axis_index(axis))
+    grown, reach = (value, 1)
+    while reach < ways:
+        theirs = lax.ppermute(grown, axis, [(d, d ^ reach) for d in range(ways)])
+        mine_first = jnp.concatenate([grown, theirs], axis=dim)
+        theirs_first = jnp.concatenate([theirs, grown], axis=dim)
+        grown = jnp.where(here & reach == 0, mine_first, theirs_first)
+        reach = 2 * reach
+    return grown
 
 
 def passed_along(value, axis, steps):
@@ -55,7 +67,7 @@
     src_float = src_spectra.astype(jnp.float32)
     src_square = 0.5 * jnp.sum(src_float * src_float, axis=0)
     src_bias = log_src_weight + src_potential
-    tgt_bias = lax.all_gather(log_tgt_weight + tgt_potential, "blk", axis=0, tiled=True)
+    tgt_bias = collect(log_tgt_weight + tgt_potential, "blk", 0)
     own_width = tgt_spectra.shape[1]
     everything = tgt_bias.shape[0]
     rows_here = src_spectra.shape[1]

time: 62.4 us -> 59.4 us (0.952)
  blocking collectives: 25.3 us -> 10.4 us
  waiting for transfers between devices: 16 us -> 22.3 us
  starting transfers between devices: 12.2 us -> 16.4 us
  local copies, waits for them, and re-layouts: 2.21 us -> 3.5 us
    all_gather x1 -> x0, blocking collectives: 14.9 us -> none  [on_device(): lax.all_gather(log_tgt_weight + tgt_potential, 'blk', axis=0, tiled=True)]
    ppermute x0 -> x2, starting transfers between devices: none -> 6.13 us  [collect(): theirs = lax.ppermute(grown, axis, [(d, d ^ reach) for d in range(ways)])]
    ppermute x0 -> x2, waiting for transfers between devices: none -> 3.15 us  [collect(): theirs = lax.ppermute(grown, axis, [(d, d ^ reach) for d in range(ways)])]
    ppermute x12, waiting for transfers between devices: 16 us -> 19.1 us  [passed_along(): return lax.ppermute(value, axis, pairs)]
    ppermute x12, starting transfers between devices: 12.2 us -> 10.3 us  [passed_along(): return lax.ppermute(value, axis, pairs)]
    slice x4 -> x6, local copies, waits for them, and re-layouts: 0.03 us -> 0.83 us  [merged(): tail = jax.tree.map(lambda part: part[1:], pieces)]
    unnamed x14 -> x16, local copies, waits for them, and re-layouts: 1.4 us -> 1.88 us
  transfers between devices with their start and end apart: 12 -> 14, of which waited for: 8 -> 10; matrix products, arithmetic and copies ran while one was open for 6% -> 7% of each run, Pallas kernels for 0% -> 0%
where the time goes in v1:
time: 59.4 us; the launch traced here: 59 us
  waiting for transfers between devices  22.3 us (38%)
  starting transfers between devices  16.4 us (28%)
  blocking collectives  10.4 us (18%)
  local copies, waits for them, and re-layouts  3.5 us (6%)
  other arithmetic  3.31 us (6%)
  matrix products  1.93 us (3%)
  between operations  0.72 us (1%)
    ppermute x12, waiting for transfers between devices, passed_along(): return lax.ppermute(value, axis, pairs)  19.1 us
    all_gather x2, blocking collectives, merged(): pieces = jax.tree.map(lambda part: lax.all_gather(part, axis), value)  10.4 us
    ppermute x12, starting transfers between devices, passed_along(): return lax.ppermute(value, axis, pairs)  10.3 us
    ppermute x2, starting transfers between devices, collect(): theirs = lax.ppermute(grown, axis, [(d, d ^ reach) for d in range(ways)])  6.13 us
    ppermute x2, waiting for transfers between devices, collect(): theirs = lax.ppermute(grown, axis, [(d, d ^ reach) for d in range(ways)])  3.15 us
    dot_general x4, matrix products, tile_scores(): lax.dot_general(src_spectra, spectra_piece, (((0,), (0,)), ((), ())), pre...  1.93 us
    unnamed x16, local copies, waits for them, and re-layouts  1.88 us
    reduce_sum x4, other arithmetic, column_part(): jnp.sum(jnp.exp(col_scores - block_peak[None, :]), axis=0)  1.74 us
  transfers between devices with their start and end apart: 14, of which 10 were waited for; matrix products, arithmetic and copies ran while one was open for 7% of the time, Pallas kernels for 0%

profile of v1, /device:TPU:0, one launch (start us, length us, event | category | flops | bytes accessed | tf_op | source)
XLA Modules:
  0.0 59.0 jit_solution(5936960070386173701)
XLA Ops:
  0.7 0.6 %copy-done.5 = f32[1024]{0:T(1024)S(1)} copy-done((f32[1024]{0:T(1024)S(1)}, f32[1024]{0:T(1024)}, u32[]{:S(2)}) %copy-start.5) | copy-done | bytes 4120
  1.3 3.1 %collective-permute-start.3 = (f32[1024]{0:T(1024)S(1)}, f32[1024]{0:T(1024)S(1)}, u32[]{:S(2)}, u32[]{:S(2)}) collective-permute-start(f32[1024]{0:T(1024)S(1)} %add.130), channel_id=1, source_target_pairs={{0,1},{1,0},{2,3},{3,2},{4,5},{5,4},{6,7},{7,6},{8,9},{9,8},{10,11... | collective-permute-start | bytes 12296 | tf_op jit(solution)/shard_map/ppermute | solution.py:11
  4.5 1.6 %collective-permute-done.3 = f32[1024]{0:T(1024)S(1)} collective-permute-done((f32[1024]{0:T(1024)S(1)}, f32[1024]{0:T(1024)S(1)}, u32[]{:S(2)}, u32[]{:S(2)}) %collective-permute-start.3) | collective-permute-done | bytes 4128 | tf_op jit(solution)/shard_map/ppermute | solution.py:11
  6.0 3.0 %collective-permute-start.4 = (f32[2048]{0:T(1024)S(1)}, f32[2048]{0:T(1024)S(1)}, u32[]{:S(2)}, u32[]{:S(2)}) collective-permute-start(f32[2048]{0:T(1024)S(1)} %maximum_select_fusion.1), channel_id=1, source_target_pairs={{0,2},{1,3},{2,0},{3,1},{4,6},{5,7},{6,4},{7,5},{8,10},{9,11},{10,... | collective-permute-start | bytes 24584 | tf_op jit(solution)/shard_map/ppermute | solution.py:11
  9.1 1.6 %collective-permute-done.4 = f32[2048]{0:T(1024)S(1)} collective-permute-done((f32[2048]{0:T(1024)S(1)}, f32[2048]{0:T(1024)S(1)}, u32[]{:S(2)}, u32[]{:S(2)}) %collective-permute-start.4) | collective-permute-done | bytes 8224 | tf_op jit(solution)/shard_map/ppermute | solution.py:11
  10.7 33.8 %while.37 = (s32[]{:T(128)}, f32[256]{0:T(256)S(1)}, f32[256]{0:T(256)S(1)}, bf16[64,1024]{1,0:T(8,128)(2,1)S(1)}, f32[1024]{0:T(1024)S(1)}, /*index=5*/f32[1024...) while((s32[]{:T(128)}, f32[256]{0:T(256)S(1)}, ...), condition=%wide.region_7.8_spmd.clone, body=%wide.region_1.7_spmd.clone.sunk | while | flops 36902160 | bytes 3297739 | solution.py:100
  10.7 2.0 %collective-permute-start = (bf16[64,1024]{1,0:T(8,128)(2,1)S(1)}, bf16[64,1024]{1,0:T(8,128)(2,1)S(1)}, u32[]{:S(2)}, u32[]{:S(2)}) collective-permute-start(bf16[64,1024]{1,0:T(8,128)(2,1)S(1)} %copy.17), channel_id=1, source_target_pairs={{0,1},{1,2},{2,3},{3,0},{4,5},{5,6},{6,7},{7,4},{8,9},{9,10},{10,1... | collective-permute-start | bytes 393224 | tf_op jit(solution)/shard_map/while/body/eval_jaxpr/ppermute | solution.py:22
  12.8 0.5 subtract_reduce_fusion.3
  13.3 0.4 exponential_reduce_fusion.3
  13.8 1.6 %collective-permute-start.1 = (f32[1024]{0:T(1024)S(1)}, f32[1024]{0:T(1024)S(1)}, u32[]{:S(2)}, u32[]{:S(2)}) collective-permute-start(f32[1024]{0:T(1024)S(1)} %get-tuple-element.501), channel_id=1, source_target_pairs={{0,1},{1,2},{2,3},{3,0},{4,5},{5,6},{6,7},{7,4},{8,9},{9,10},{10,1... | collective-permute-start | bytes 12296 | tf_op jit(solution)/shard_map/while/body/eval_jaxpr/ppermute | solution.py:22
  15.4 1.6 %collective-permute-start.2 = (f32[1024]{0:T(1024)S(1)}, f32[1024]{0:T(1024)S(1)}, u32[]{:S(2)}, u32[]{:S(2)}) collective-permute-start(f32[1024]{0:T(1024)S(1)} %get-tuple-element.502), channel_id=1, source_target_pairs={{0,1},{1,2},{2,3},{3,0},{4,5},{5,6},{6,7},{7,4},{8,9},{9,10},{10,1... | collective-permute-start | bytes 12296 | tf_op jit(solution)/shard_map/while/body/eval_jaxpr/ppermute | solution.py:22
  17.0 2.2 %collective-permute-done.1 = f32[1024]{0:T(1024)S(1)} collective-permute-done((f32[1024]{0:T(1024)S(1)}, f32[1024]{0:T(1024)S(1)}, u32[]{:S(2)}, u32[]{:S(2)}) %collective-permute-start.1) | collective-permute-done | bytes 4128 | tf_op jit(solution)/shard_map/while/body/eval_jaxpr/ppermute | solution.py:22
  19.2 1.6 %collective-permute-done.2 = f32[1024]{0:T(1024)S(1)} collective-permute-done((f32[1024]{0:T(1024)S(1)}, f32[1024]{0:T(1024)S(1)}, u32[]{:S(2)}, u32[]{:S(2)}) %collective-permute-start.2) | collective-permute-done | bytes 4128 | tf_op jit(solution)/shard_map/while/body/eval_jaxpr/ppermute | solution.py:22
  21.0 0.5 subtract_reduce_fusion.3
  22.0 1.5 %collective-permute-start.2 = (f32[1024]{0:T(1024)S(1)}, f32[1024]{0:T(1024)S(1)}, u32[]{:S(2)}, u32[]{:S(2)}) collective-permute-start(f32[1024]{0:T(1024)S(1)} %get-tuple-element.502), channel_id=1, source_target_pairs={{0,1},{1,2},{2,3},{3,0},{4,5},{5,6},{6,7},{7,4},{8,9},{9,10},{10,1... | collective-permute-start | bytes 12296 | tf_op jit(solution)/shard_map/while/body/eval_jaxpr/ppermute | solution.py:22
  23.6 4.6 %collective-permute-done.1 = f32[1024]{0:T(1024)S(1)} collective-permute-done((f32[1024]{0:T(1024)S(1)}, f32[1024]{0:T(1024)S(1)}, u32[]{:S(2)}, u32[]{:S(2)}) %collective-permute-start.1) | collective-permute-done | bytes 4128 | tf_op jit(solution)/shard_map/while/body/eval_jaxpr/ppermute | solution.py:22
  28.4 0.5 subtract_reduce_fusion.3
  29.4 2.3 %collective-permute-start.1 = (f32[1024]{0:T(1024)S(1)}, f32[1024]{0:T(1024)S(1)}, u32[]{:S(2)}, u32[]{:S(2)}) collective-permute-start(f32[1024]{0:T(1024)S(1)} %get-tuple-element.501), channel_id=1, source_target_pairs={{0,1},{1,2},{2,3},{3,0},{4,5},{5,6},{6,7},{7,4},{8,9},{9,10},{10,1... | collective-permute-start | bytes 12296 | tf_op jit(solution)/shard_map/while/body/eval_jaxpr/ppermute | solution.py:22
  31.8 3.8 %collective-permute-done.1 = f32[1024]{0:T(1024)S(1)} collective-permute-done((f32[1024]{0:T(1024)S(1)}, f32[1024]{0:T(1024)S(1)}, u32[]{:S(2)}, u32[]{:S(2)}) %collective-permute-start.1) | collective-permute-done | bytes 4128 | tf_op jit(solution)/shard_map/while/body/eval_jaxpr/ppermute | solution.py:22
  35.6 1.5 %collective-permute-done.2 = f32[1024]{0:T(1024)S(1)} collective-permute-done((f32[1024]{0:T(1024)S(1)}, f32[1024]{0:T(1024)S(1)}, u32[]{:S(2)}, u32[]{:S(2)}) %collective-permute-start.2) | collective-permute-done | bytes 4128 | tf_op jit(solution)/shard_map/while/body/eval_jaxpr/ppermute | solution.py:22
  37.3 0.5 subtract_reduce_fusion.3
  38.3 0.9 %collective-permute-start.1 = (f32[1024]{0:T(1024)S(1)}, f32[1024]{0:T(1024)S(1)}, u32[]{:S(2)}, u32[]{:S(2)}) collective-permute-start(f32[1024]{0:T(1024)S(1)} %get-tuple-element.501), channel_id=1, source_target_pairs={{0,1},{1,2},{2,3},{3,0},{4,5},{5,6},{6,7},{7,4},{8,9},{9,10},{10,1... | collective-permute-start | bytes 12296 | tf_op jit(solution)/shard_map/while/body/eval_jaxpr/ppermute | solution.py:22
  39.2 4.7 %collective-permute-done.1 = f32[1024]{0:T(1024)S(1)} collective-permute-done((f32[1024]{0:T(1024)S(1)}, f32[1024]{0:T(1024)S(1)}, u32[]{:S(2)}, u32[]{:S(2)}) %collective-permute-start.1) | collective-permute-done | bytes 4128 | tf_op jit(solution)/shard_map/while/body/eval_jaxpr/ppermute | solution.py:22
  44.0 0.6 collective-permute-done.2
  44.6 5.2 %all-gather = f32[4096]{0:T(1024)S(1)} all-gather(f32[1024]{0:T(1024)S(1)} %get-tuple-element.300), channel_id=2, replica_groups=mesh['pair'=2,'rep'=4,'blk'=4] {'rep'}, dimensions={0}, use_global_device_ids=true | all-gather | bytes 20480 | tf_op jit(solution)/shard_map/all_gather | solution.py:26
  49.8 0.6 %copy-done.1 = f32[4096]{0:T(1024)} copy-done((f32[4096]{0:T(1024)}, f32[4096]{0:T(1024)S(1)}, u32[]{:S(2)}) %copy-start.1) | copy-done | bytes 16408
  50.4 5.2 %all-gather.1 = f32[4096]{0:T(1024)S(1)} all-gather(f32[1024]{0:T(1024)S(1)} %get-tuple-element.301), channel_id=3, replica_groups=mesh['pair'=2,'rep'=4,'blk'=4] {'rep'}, dimensions={0}, use_global_device_ids=true | all-gather | bytes 20480 | tf_op jit(solution)/shard_map/all_gather | solution.py:26
  55.6 0.6 %copy-done.2 = f32[4096]{0:T(1024)} copy-done((f32[4096]{0:T(1024)}, f32[4096]{0:T(1024)S(1)}, u32[]{:S(2)}) %copy-start.2) | copy-done | bytes 16408
  56.3 0.7 %slice-done.2 = f32[3072]{0:T(1024)S(1)} async-done(((f32[4096]{0:T(1024)}), f32[3072]{0:T(1024)S(1)}, s32[]{:S(2)}) %slice-start.2) | async-done | bytes 12312 | tf_op jit(solution)/shard_map/slice | solution.py:28
  57.0 0.7 %slice-done.1 = f32[1024]{0:T(1024)S(1)} async-done(((f32[4096]{0:T(1024)}), f32[1024]{0:T(1024)S(1)}, s32[]{:S(2)}) %slice-start.1) | async-done | bytes 4120 | tf_op jit(solution)/shard_map/slice | solution.py:27
  57.8 0.6 %add_multiply_fusion = f32[1024]{0:T(1024)} fusion(f32[1024]{0:T(1024)S(1)} %copy-done.4, f32[1024]{0:T(1024)S(1)} %get-tuple-element.302, f32[1024]{0:T(1024)S(1)} %get-tuple-element.303), kind=kLoop, calls=%fused_computation.18 | loop fusion | flops 4096 | bytes 16384 | tf_op jit(solution)/shard_map/mul | solution.py:106
  58.4 0.6 add_multiply_fusion.1
  (84 shorter events, 2.6 us)
Async XLA Ops:
  0.6 0.7 %copy-start.5 = (f32[1024]{0:T(1024)S(1)}, f32[1024]{0:T(1024)}, u32[]{:S(2)}) copy-start(f32[1024]{0:T(1024)} %param.13) | copy-start | bytes 12292
  0.6 0.7 %copy-start.4 = (f32[1024]{0:T(1024)S(1)}, f32[1024]{0:T(1024)}, u32[]{:S(2)}) copy-start(f32[1024]{0:T(1024)} %param.15) | copy-start | bytes 12292
  0.7 3.8 %copy-start.3 = (bf16[64,256]{1,0:T(8,128)(2,1)S(1)}, bf16[64,256]{1,0:T(8,128)(2,1)}, u32[]{:S(2)}) copy-start(bf16[64,256]{1,0:T(8,128)(2,1)} %param.10) | copy-start | bytes 98308
  0.7 8.4 %copy-start.6 = (f32[256]{0:T(256)S(1)}, f32[256]{0:T(256)}, u32[]{:S(2)}) copy-start(f32[256]{0:T(256)} %param.14) | copy-start | bytes 3076
  0.7 8.4 %copy-start.7 = (f32[256]{0:T(256)S(1)}, f32[256]{0:T(256)}, u32[]{:S(2)}) copy-start(f32[256]{0:T(256)} %param.12) | copy-start | bytes 3076
  1.3 9.4 %copy-start = (bf16[64,1024]{1,0:T(8,128)(2,1)S(1)}, bf16[64,1024]{1,0:T(8,128)(2,1)}, u32[]{:S(2)}) copy-start(bf16[64,1024]{1,0:T(8,128)(2,1)} %param.11) | copy-start | bytes 393220
  1.3 4.7 %collective-permute-start.3 = (f32[1024]{0:T(1024)S(1)}, f32[1024]{0:T(1024)S(1)}, u32[]{:S(2)}, u32[]{:S(2)}) collective-permute-start(f32[1024]{0:T(1024)S(1)} %add.130), channel_id=1, source_target_pairs={{0,1},{1,0},{2,3},{3,2},{4,5},{5,4},{6,7},{7,6},{8,9},{9,8},{10,11... | collective-permute-start | bytes 12296 | tf_op jit(solution)/shard_map/ppermute | solution.py:11
  6.0 4.7 %collective-permute-start.4 = (f32[2048]{0:T(1024)S(1)}, f32[2048]{0:T(1024)S(1)}, u32[]{:S(2)}, u32[]{:S(2)}) collective-permute-start(f32[2048]{0:T(1024)S(1)} %maximum_select_fusion.1), channel_id=1, source_target_pairs={{0,2},{1,3},{2,0},{3,1},{4,6},{5,7},{6,4},{7,5},{8,10},{9,11},{10,... | collective-permute-start | bytes 24584 | tf_op jit(solution)/shard_map/ppermute | solution.py:11
  10.7 10.1 %collective-permute-start = (bf16[64,1024]{1,0:T(8,128)(2,1)S(1)}, bf16[64,1024]{1,0:T(8,128)(2,1)S(1)}, u32[]{:S(2)}, u32[]{:S(2)}) collective-permute-start(bf16[64,1024]{1,0:T(8,128)(2,1)S(1)} %copy.17), channel_id=1, source_target_pairs={{0,1},{1,2},{2,3},{3,0},{4,5},{5,6},{6,7},{7,4},{8,9},{9,10},{10,1... | collective-permute-start | bytes 393224 | tf_op jit(solution)/shard_map/while/body/eval_jaxpr/ppermute | solution.py:22
  13.8 5.5 %collective-permute-start.1 = (f32[1024]{0:T(1024)S(1)}, f32[1024]{0:T(1024)S(1)}, u32[]{:S(2)}, u32[]{:S(2)}) collective-permute-start(f32[1024]{0:T(1024)S(1)} %get-tuple-element.501), channel_id=1, source_target_pairs={{0,1},{1,2},{2,3},{3,0},{4,5},{5,6},{6,7},{7,4},{8,9},{9,10},{10,1... | collective-permute-start | bytes 12296 | tf_op jit(solution)/shard_map/while/body/eval_jaxpr/ppermute | solution.py:22
  15.4 5.4 %collective-permute-start.2 = (f32[1024]{0:T(1024)S(1)}, f32[1024]{0:T(1024)S(1)}, u32[]{:S(2)}, u32[]{:S(2)}) collective-permute-start(f32[1024]{0:T(1024)S(1)} %get-tuple-element.502), channel_id=1, source_target_pairs={{0,1},{1,2},{2,3},{3,0},{4,5},{5,6},{6,7},{7,4},{8,9},{9,10},{10,1... | collective-permute-start | bytes 12296 | tf_op jit(solution)/shard_map/while/body/eval_jaxpr/ppermute | solution.py:22
  20.8 7.4 %collective-permute-start = (bf16[64,1024]{1,0:T(8,128)(2,1)S(1)}, bf16[64,1024]{1,0:T(8,128)(2,1)S(1)}, u32[]{:S(2)}, u32[]{:S(2)}) collective-permute-start(bf16[64,1024]{1,0:T(8,128)(2,1)S(1)} %copy.17), channel_id=1, source_target_pairs={{0,1},{1,2},{2,3},{3,0},{4,5},{5,6},{6,7},{7,4},{8,9},{9,10},{10,1... | collective-permute-start | bytes 393224 | tf_op jit(solution)/shard_map/while/body/eval_jaxpr/ppermute | solution.py:22
  22.0 6.2 %collective-permute-start.1 = (f32[1024]{0:T(1024)S(1)}, f32[1024]{0:T(1024)S(1)}, u32[]{:S(2)}, u32[]{:S(2)}) collective-permute-start(f32[1024]{0:T(1024)S(1)} %get-tuple-element.501), channel_id=1, source_target_pairs={{0,1},{1,2},{2,3},{3,0},{4,5},{5,6},{6,7},{7,4},{8,9},{9,10},{10,1... | collective-permute-start | bytes 12296 | tf_op jit(solution)/shard_map/while/body/eval_jaxpr/ppermute | solution.py:22
  22.0 6.2 %collective-permute-start.2 = (f32[1024]{0:T(1024)S(1)}, f32[1024]{0:T(1024)S(1)}, u32[]{:S(2)}, u32[]{:S(2)}) collective-permute-start(f32[1024]{0:T(1024)S(1)} %get-tuple-element.502), channel_id=1, source_target_pairs={{0,1},{1,2},{2,3},{3,0},{4,5},{5,6},{6,7},{7,4},{8,9},{9,10},{10,1... | collective-permute-start | bytes 12296 | tf_op jit(solution)/shard_map/while/body/eval_jaxpr/ppermute | solution.py:22
  28.3 8.9 %collective-permute-start = (bf16[64,1024]{1,0:T(8,128)(2,1)S(1)}, bf16[64,1024]{1,0:T(8,128)(2,1)S(1)}, u32[]{:S(2)}, u32[]{:S(2)}) collective-permute-start(bf16[64,1024]{1,0:T(8,128)(2,1)S(1)} %copy.17), channel_id=1, source_target_pairs={{0,1},{1,2},{2,3},{3,0},{4,5},{5,6},{6,7},{7,4},{8,9},{9,10},{10,1... | collective-permute-start | bytes 393224 | tf_op jit(solution)/shard_map/while/body/eval_jaxpr/ppermute | solution.py:22
  29.4 6.2 %collective-permute-start.1 = (f32[1024]{0:T(1024)S(1)}, f32[1024]{0:T(1024)S(1)}, u32[]{:S(2)}, u32[]{:S(2)}) collective-permute-start(f32[1024]{0:T(1024)S(1)} %get-tuple-element.501), channel_id=1, source_target_pairs={{0,1},{1,2},{2,3},{3,0},{4,5},{5,6},{6,7},{7,4},{8,9},{9,10},{10,1... | collective-permute-start | bytes 12296 | tf_op jit(solution)/shard_map/while/body/eval_jaxpr/ppermute | solution.py:22
  31.7 5.4 %collective-permute-start.2 = (f32[1024]{0:T(1024)S(1)}, f32[1024]{0:T(1024)S(1)}, u32[]{:S(2)}, u32[]{:S(2)}) collective-permute-start(f32[1024]{0:T(1024)S(1)} %get-tuple-element.502), channel_id=1, source_target_pairs={{0,1},{1,2},{2,3},{3,0},{4,5},{5,6},{6,7},{7,4},{8,9},{9,10},{10,1... | collective-permute-start | bytes 12296 | tf_op jit(solution)/shard_map/while/body/eval_jaxpr/ppermute | solution.py:22
  37.1 7.4 %collective-permute-start = (bf16[64,1024]{1,0:T(8,128)(2,1)S(1)}, bf16[64,1024]{1,0:T(8,128)(2,1)S(1)}, u32[]{:S(2)}, u32[]{:S(2)}) collective-permute-start(bf16[64,1024]{1,0:T(8,128)(2,1)S(1)} %copy.17), channel_id=1, source_target_pairs={{0,1},{1,2},{2,3},{3,0},{4,5},{5,6},{6,7},{7,4},{8,9},{9,10},{10,1... | collective-permute-start | bytes 393224 | tf_op jit(solution)/shard_map/while/body/eval_jaxpr/ppermute | solution.py:22
  38.3 5.7 %collective-permute-start.1 = (f32[1024]{0:T(1024)S(1)}, f32[1024]{0:T(1024)S(1)}, u32[]{:S(2)}, u32[]{:S(2)}) collective-permute-start(f32[1024]{0:T(1024)S(1)} %get-tuple-element.501), channel_id=1, source_target_pairs={{0,1},{1,2},{2,3},{3,0},{4,5},{5,6},{6,7},{7,4},{8,9},{9,10},{10,1... | collective-permute-start | bytes 12296 | tf_op jit(solution)/shard_map/while/body/eval_jaxpr/ppermute | solution.py:22
  39.1 5.4 %collective-permute-start.2 = (f32[1024]{0:T(1024)S(1)}, f32[1024]{0:T(1024)S(1)}, u32[]{:S(2)}, u32[]{:S(2)}) collective-permute-start(f32[1024]{0:T(1024)S(1)} %get-tuple-element.502), channel_id=1, source_target_pairs={{0,1},{1,2},{2,3},{3,0},{4,5},{5,6},{6,7},{7,4},{8,9},{9,10},{10,1... | collective-permute-start | bytes 12296 | tf_op jit(solution)/shard_map/while/body/eval_jaxpr/ppermute | solution.py:22
  49.8 0.6 %copy-start.1 = (f32[4096]{0:T(1024)}, f32[4096]{0:T(1024)S(1)}, u32[]{:S(2)}) copy-start(f32[4096]{0:T(1024)S(1)} %all-gather) | copy-start | bytes 49156
  55.5 0.6 %copy-start.2 = (f32[4096]{0:T(1024)}, f32[4096]{0:T(1024)S(1)}, u32[]{:S(2)}) copy-start(f32[4096]{0:T(1024)S(1)} %all-gather.1) | copy-start | bytes 49156
  55.5 0.7 %slice-start = ((f32[4096]{0:T(1024)}), f32[3072]{0:T(1024)S(1)}, s32[]{:S(2)}) async-start(f32[4096]{0:T(1024)} %copy-done.1), calls=%async_computation | async-start | bytes 24576 | tf_op jit(solution)/shard_map/slice | solution.py:28
  56.3 0.7 %slice-start.2 = ((f32[4096]{0:T(1024)}), f32[3072]{0:T(1024)S(1)}, s32[]{:S(2)}) async-start(f32[4096]{0:T(1024)} %copy-done.2), calls=%async_computation.2 | async-start | bytes 24576 | tf_op jit(solution)/shard_map/slice | solution.py:28
  57.0 0.7 %slice-start.1 = ((f32[4096]{0:T(1024)}), f32[1024]{0:T(1024)S(1)}, s32[]{:S(2)}) async-start(f32[4096]{0:T(1024)} %copy-done.1), calls=%async_computation.1 | async-start | bytes 8192 | tf_op jit(solution)/shard_map/slice | solution.py:27
  57.0 0.7 %slice-start.3 = ((f32[4096]{0:T(1024)}), f32[1024]{0:T(1024)S(1)}, s32[]{:S(2)}) async-start(f32[4096]{0:T(1024)} %copy-done.2), calls=%async_computation.3 | async-start | bytes 8192 | tf_op jit(solution)/shard_map/slice | solution.py:27
